TPU v7x, 32 devices: a whole 2x2x4 slice. The times are simulated.
32 devices in a mesh: groups: 2 (over y), ctx: 4 (over x, core), head: 4 (over z).
Axes of the slice: x: 2, y: 2, z: 4, core: 2. Of those that a mesh axis runs over, the one named last changes fastest.
Arguments:
- queries: bfloat16 [384, 64, 128], P(('groups', 'ctx'), 'head'), parts along dimension 0, may hold values from -16 to 16
- prefix_keys: bfloat16 [16384, 8, 128], P(('groups', 'ctx'), 'head'), parts along dimension 0, may hold values from -16 to 16
- prefix_values: bfloat16 [16384, 8, 128], P(('groups', 'ctx'), 'head'), parts along dimension 0, may hold values from -12 to 12
- suffix_keys: bfloat16 [384, 512, 8, 128], P(('groups', 'ctx'), None, 'head'), parts along dimension 0, may hold values from -16 to 16
- suffix_values: bfloat16 [384, 512, 8, 128], P(('groups', 'ctx'), None, 'head'), parts along dimension 0, may hold values from -12 to 12
- lengths: int32 [384], P(('groups', 'ctx')), parts along dimension 0, may hold values from 1 to 512, as said below
Outputs:
- attended: bfloat16 [384, 64, 128], P(('groups', 'ctx'), 'head'), parts along dimension 0
There are 2 independent parts, one for each index of `groups`. A program takes and returns all parts, laid end to end along the dimension named above; each array names one. Nothing has to cross between parts.
Inputs may be any that keep to these rules, and one draw needn't show every extreme that they name: The live slots of a row are its first lengths[r] slots; some row of each part has exactly 512.
All inputs are finite; a program needn't handle non-finite values.
Results may differ from a plain program's by a relative error of at most 0.0025.
Values may be sent and summed in bfloat16 or wider, within the bound.
A program may use at most 128 MiB of HBM per device.

v0:
```python
import jax
import jax.numpy as jnp
from jax import lax
from jax.sharding import PartitionSpec as P


def shards(queries, prefix_keys, prefix_values, suffix_keys, suffix_values, lengths):
    rows_dev, heads_local, head_width = queries.shape
    kv_local = prefix_keys.shape[1]
    group_size = heads_local // kv_local
    span = suffix_keys.shape[1]
    scaling = head_width ** (-0.5)
    ctx_count = lax.axis_size("ctx")
    every_query = lax.all_gather(queries, "ctx", axis=0, tiled=True)
    all_rows = every_query.shape[0]
    shards_per = max(1, min(ctx_count, 1024 // max(1, rows_dev * group_size)))
    while ctx_count % shards_per:
        shards_per -= 1
    block_rows = rows_dev * shards_per
    block_count = all_rows // block_rows
    blocked = every_query.reshape(block_count, block_rows, kv_local, group_size, head_width)

    def block_terms(row_block):
        scores = (
            jnp.einsum("rkgd,pkd->rkgp", row_block, prefix_keys, preferred_element_type=jnp.float32)
            * scaling
        )
        local_top = jnp.max(scores, axis=-1)
        weights = jnp.exp(scores - local_top[..., None]).astype(jnp.bfloat16)
        sums_now = jnp.sum(weights, axis=-1, dtype=jnp.float32)
        accum_now = jnp.einsum(
            "rkgp,pkd->rkgd", weights, prefix_values, preferred_element_type=jnp.float32
        )
        return (local_top, sums_now, accum_now)

    prefix_top, prefix_sum, prefix_accum = lax.map(block_terms, blocked)
    prefix_top = prefix_top.reshape(all_rows, kv_local, group_size)
    prefix_sum = prefix_sum.reshape(all_rows, kv_local, group_size)
    prefix_accum = prefix_accum.reshape(all_rows, kv_local, group_size, head_width)
    own_query = queries.reshape(rows_dev, kv_local, group_size, head_width)
    start_row = lax.axis_index("ctx") * rows_dev
    positions = jnp.arange(span, dtype=jnp.int32)
    live_all = (positions[None, :] < lengths[:, None])[:, None, None, :]
    suffix_scores = (
        jnp.einsum("rkgd,rskd->rkgs", own_query, suffix_keys, preferred_element_type=jnp.float32)
        * scaling
    )
    suffix_top = jnp.max(jnp.where(live_all, suffix_scores, -jnp.inf), axis=-1)
    own_prefix_top = lax.dynamic_slice_in_dim(prefix_top, start_row, rows_dev, 0)
    merged_top = lax.dynamic_update_slice_in_dim(
        prefix_top, jnp.maximum(own_prefix_top, suffix_top), start_row, 0
    )
    row_top = lax.pmax(merged_top, "ctx")
    own_top = lax.dynamic_slice_in_dim(row_top, start_row, rows_dev, 0)
    weights = jnp.where(live_all, jnp.exp(suffix_scores - own_top[..., None]), 0.0).astype(
        jnp.bfloat16
    )
    sums_now = jnp.sum(weights, axis=-1, dtype=jnp.float32)
    accum_now = jnp.einsum(
        "rkgs,rskd->rkgd", weights, suffix_values, preferred_element_type=jnp.float32
    )
    block_scale = jnp.exp(prefix_top - row_top)
    prefix_sum = prefix_sum * block_scale
    prefix_accum = prefix_accum * block_scale[..., None]
    full_sum, full_accum = lax.psum((prefix_sum, prefix_accum), "ctx")
    shared_sum = lax.dynamic_slice_in_dim(full_sum, start_row, rows_dev, 0)
    shared_accum = lax.dynamic_slice_in_dim(full_accum, start_row, rows_dev, 0)
    weight_sum = shared_sum + sums_now
    attended = ((shared_accum + accum_now) / weight_sum[..., None]).astype(jnp.bfloat16)
    return attended.reshape(rows_dev, heads_local, head_width)


def solution(mesh):
    placed = (
        P(("groups", "ctx"), "head", None),
        P(("groups", "ctx"), "head", None),
        P(("groups", "ctx"), "head", None),
        P(("groups", "ctx"), None, "head", None),
        P(("groups", "ctx"), None, "head", None),
        P(("groups", "ctx")),
    )
    return jax.shard_map(
        shards,
        mesh=mesh,
        in_specs=placed,
        out_specs=P(("groups", "ctx"), "head", None),
        check_vma=False,
    )
```

profile of v0, /device:TPU:0, one launch (start us, length us, event | category | flops | bytes accessed | tf_op | source)
XLA Modules:
  0.0 136.4 jit_solution(2666634758440160694)
XLA Ops:
  6.5 10.4 %all_gather.3 = bf16[192,16,128]{2,1,0:T(8,128)(2,1)S(1)} all-gather(bf16[48,16,128]{2,1,0:T(8,128)(2,1)} %param.8), channel_id=1, replica_groups=mesh['groups'=2,'ctx'=4,'head'=4] {'ctx'}, dimensions={0}, use_global_device_ids=true | all-gather | bytes 983040 | tf_op jit(solution)/shard_map/all_gather | solution.py:14
  16.9 1.4 copy.38
  18.3 0.1 copy.39
  18.5 39.7 %while.14 = (s32[]{:T(128)}, f32[2,96,2,8]{1,0,3,2:T(2,128)S(1)}, f32[2,96,2,8]{1,0,3,2:T(2,128)S(1)}, f32[2,96,2,8,128]{4,3,2,1,0:T(8,128)}, bf16[2,96,2,8,128]...) while((s32[]{:T(128)}, f32[2,96,2,8]{1,0,3,2:T(2,128)S(1)}, ...), condition=%wide.region_3.4_spmd, body=%wide.region_0.3_spmd.sunk | while | flops 1642066944 | bytes 55255212 | solution.py:36
  18.5 6.4 %bitcast_reduce_fusion.2 = (f32[96,2,8]{2,0,1:T(8,128)S(1)}, f32[2,96,8,2048]{3,2,1,0:T(8,128)}) fusion(bf16[2048,2,128]{2,0,1:T(8,128)(2,1)S(1)} %get-tuple-element.165, bf16[2,96,2,8,128]{4,3,2,1,0:T(8,128)(2,1)S(1)} %get-tuple-element.164, s32[]{:T(128)S(6)} %copy.94), kind=kOutput, calls=%fused_computation.1.clone.1 | convolution fusion | flops 811596288 | bytes 14030852 | tf_op jit(solution)/shard_map/while/body/eval_jaxpr/rkgd,pkd->rkgp/dot_general | solution.py:25
  25.0 6.1 %convert_reduce_fusion.3 = f32[96,2,8]{2,0,1:T(8,128)S(1)} fusion(f32[96,2,8]{2,0,1:T(8,128)S(1)} %get-tuple-element.140, f32[2,96,8,2048]{3,2,1,0:T(8,128)} %get-tuple-element.141), kind=kLoop, calls=%fused_computation.4.clone.1 | loop fusion | flops 15727104 | bytes 12595200 | tf_op jit(solution)/shard_map/while/body/eval_jaxpr/reduce_sum | solution.py:30
  31.3 5.8 %convolution_bitcast_fusion.2 = f32[1,96,2,8,128]{4,3,1,2,0:T(8,128)S(1)} fusion(bf16[2048,2,128]{2,0,1:T(8,128)(2,1)S(1)} %get-tuple-element.166, f32[2,96,8,2048]{3,2,1,0:T(8,128)} %get-tuple-element.141, f32[96,2,8]{2,0,1:T(8,128)S(1)} %get-tuple-element.140), kind=kOutput, calls=%fused_computation.5.clone.1 | convolution fusion | flops 814743552 | bytes 14424064 | tf_op jit(solution)/shard_map/while/body/eval_jaxpr/rkgp,pkd->rkgd/dot_general | solution.py:31
  37.2 1.2 copy-done.1
  38.4 6.4 %bitcast_reduce_fusion.2 = (f32[96,2,8]{2,0,1:T(8,128)S(1)}, f32[2,96,8,2048]{3,2,1,0:T(8,128)}) fusion(bf16[2048,2,128]{2,0,1:T(8,128)(2,1)S(1)} %get-tuple-element.165, bf16[2,96,2,8,128]{4,3,2,1,0:T(8,128)(2,1)S(1)} %get-tuple-element.164, s32[]{:T(128)S(6)} %copy.94), kind=kOutput, calls=%fused_computation.1.clone.1 | convolution fusion | flops 811596288 | bytes 14030852 | tf_op jit(solution)/shard_map/while/body/eval_jaxpr/rkgd,pkd->rkgp/dot_general | solution.py:25
  44.9 6.1 %convert_reduce_fusion.3 = f32[96,2,8]{2,0,1:T(8,128)S(1)} fusion(f32[96,2,8]{2,0,1:T(8,128)S(1)} %get-tuple-element.140, f32[2,96,8,2048]{3,2,1,0:T(8,128)} %get-tuple-element.141), kind=kLoop, calls=%fused_computation.4.clone.1 | loop fusion | flops 15727104 | bytes 12595200 | tf_op jit(solution)/shard_map/while/body/eval_jaxpr/reduce_sum | solution.py:30
  51.1 5.8 %convolution_bitcast_fusion.2 = f32[1,96,2,8,128]{4,3,1,2,0:T(8,128)S(1)} fusion(bf16[2048,2,128]{2,0,1:T(8,128)(2,1)S(1)} %get-tuple-element.166, f32[2,96,8,2048]{3,2,1,0:T(8,128)} %get-tuple-element.141, f32[96,2,8]{2,0,1:T(8,128)S(1)} %get-tuple-element.140), kind=kOutput, calls=%fused_computation.5.clone.1 | convolution fusion | flops 814743552 | bytes 14424064 | tf_op jit(solution)/shard_map/while/body/eval_jaxpr/rkgp,pkd->rkgd/dot_general | solution.py:31
  57.0 1.2 copy-done.1
  58.4 0.1 iota_compare_fusion
  58.5 6.7 %select_reduce_fusion = (f32[48,2,8]{2,1,0:T(2,128)S(1)}, f32[48,2,8,512]{3,2,1,0:T(8,128)S(1)}) fusion(pred[48,512]{1,0:T(8,128)(4,1)S(1)} %iota_compare_fusion, bf16[48,512,2,128]{3,2,1,0:T(2,128)(2,1)} %param.11, bf16[48,16,128]{2,1,0:T(8,128)(2,1)S(1)} %copy-done.4), kind=kOutput, calls=%fused_computation.20 | convolution fusion | flops 101842176 | bytes 14380032 | tf_op jit(solution)/shard_map/rkgd,rskd->rkgs/dot_general | solution.py:45
  65.3 0.2 dynamic_update_slice.14
  65.5 11.2 %pmax.7 = f32[192,2,8]{0,2,1:T(8,128)S(1)} all-reduce(f32[192,2,8]{0,2,1:T(8,128)S(1)} %dynamic_update_slice.14), channel_id=1, replica_groups=mesh['groups'=2,'ctx'=4,'head'=4] {'ctx'}, use_global_device_ids=true, to_apply=%region_5.6 | all-reduce | flops 3072 | bytes 24576 | tf_op jit(solution)/shard_map/pmax | solution.py:53
  76.7 0.2 copy.44
  76.9 1.6 %bitcast_multiply_fusion = f32[192,2,8,128]{3,2,1,0:T(8,128)} fusion(f32[2,96,2,8,128]{4,3,2,1,0:T(8,128)S(1)} %copy-done.2, f32[192,2,8]{2,1,0:T(2,128)S(1)} %copy.44), kind=kLoop, calls=%fused_computation.17 | loop fusion | flops 393216 | bytes 3158016 | tf_op jit(solution)/shard_map/mul | solution.py:64
  78.6 0.1 copy.45
  78.7 0.6 convert_reduce_fusion.1
  79.3 10.9 %psum.15 = f32[192,2,8]{0,2,1:T(8,128)S(1)} all-reduce(f32[192,2,8]{0,2,1:T(8,128)S(1)} %get-tuple-element.89), channel_id=1, replica_groups=mesh['groups'=2,'ctx'=4,'head'=4] {'ctx'}, use_global_device_ids=true, to_apply=%region_7.8 | all-reduce | flops 3072 | bytes 24576 | tf_op jit(solution)/shard_map/psum | solution.py:65
  90.3 0.1 copy.49
  90.4 32.0 %all-reduce.2.cloned.1.call-done = f32[192,2,8,128]{3,2,1,0:T(8,128)} async-done(((f32[192,2,8,128]{3,2,1,0:T(8,128)}), f32[192,2,8,128]{3,2,1,0:T(8,128)}) %all-reduce.2.cloned.1.call-update) | async-done | bytes 1572880 | tf_op jit(solution)/shard_map/psum | solution.py:65
  122.4 7.1 %fusion.20 = bf16[48,16,128]{2,1,0:T(8,128)(2,1)} fusion(bf16[48,512,2,128]{3,2,1,0:T(2,128)(2,1)} %param.12, f32[192,2,8,128]{3,2,1,0:T(8,128)} %all-reduce.2.cloned.1.call-done, s32[]{:T(128)S(6)} %select_n.14, f32[48,2,8]{2,1,0:T(2,128)S(1)} %copy.49, f32[48,2,8,512]{3,2,1,0:T(8,128)S(1)} %get-tuple-element.94, f32[48,2,8]{2,1,0:T(2,128)S(1)} %copy.45, ...), kind=kOutput, calls=%fused_computation.24 | convolution fusion | flops 102531072 | bytes 14776324 | tf_op jit(solution)/shard_map/rkgs,rskd->rkgd/dot_general | solution.py:59
  (38 shorter events, 1.2 us)
Async XLA Ops:
  6.5 115.8 %all-reduce.2.cloned.1.call-start = ((), (), s32[]{:S(2)}) async-start(), calls=%async_computation | async-start | bytes 3145728 | tf_op jit(solution)/shard_map/psum | solution.py:65
  6.5 11.8 %copy-start.3 = (bf16[2048,2,128]{2,1,0:T(2,128)(2,1)S(1)}, bf16[2048,2,128]{2,1,0:T(2,128)(2,1)}, u32[]{:S(2)}) copy-start(bf16[2048,2,128]{2,1,0:T(2,128)(2,1)} %param.10) | copy-start | bytes 3145732
  18.5 39.9 %copy-start.5 = (s32[48]{0:T(128)S(1)}, s32[48]{0:T(128)}, u32[]{:S(2)}) copy-start(s32[48]{0:T(128)} %param.13) | copy-start | bytes 580
  18.5 40.0 %copy-start.4 = (bf16[48,16,128]{2,1,0:T(8,128)(2,1)S(1)}, bf16[48,16,128]{2,1,0:T(8,128)(2,1)}, u32[]{:S(2)}) copy-start(bf16[48,16,128]{2,1,0:T(8,128)(2,1)} %param.8) | copy-start | bytes 589828
  31.3 5.8 %copy-start = (f32[2,96,2,8,128]{4,3,2,1,0:T(8,128)S(1)}, f32[2,96,2,8,128]{4,3,2,1,0:T(8,128)}, u32[]{:S(2)}) copy-start(f32[2,96,2,8,128]{4,3,2,1,0:T(8,128)} %get-tuple-element.154) | copy-start | bytes 4718596 | tf_op jit(solution)/shard_map/while
  37.2 1.2 copy-start.1
  51.1 5.8 %copy-start = (f32[2,96,2,8,128]{4,3,2,1,0:T(8,128)S(1)}, f32[2,96,2,8,128]{4,3,2,1,0:T(8,128)}, u32[]{:S(2)}) copy-start(f32[2,96,2,8,128]{4,3,2,1,0:T(8,128)} %get-tuple-element.154) | copy-start | bytes 4718596 | tf_op jit(solution)/shard_map/while
  57.0 1.2 copy-start.1
  58.5 18.4 %copy-start.2 = (f32[2,96,2,8,128]{4,3,2,1,0:T(8,128)S(1)}, f32[2,96,2,8,128]{4,3,2,1,0:T(8,128)}, u32[]{:S(2)}) copy-start(f32[2,96,2,8,128]{4,3,2,1,0:T(8,128)} %get-tuple-element.44) | copy-start | bytes 4718596
Sparse Core Ops, SparseCore 0:
  78.6 43.6 all-reduce.1
where the time goes:
time: 137 us; the launch traced here: 136 us
  matrix products  38.1 us (28%)
  blocking collectives  32.5 us (24%)
  waiting for transfers between devices  32 us (23%)
  other arithmetic  14.7 us (11%)
  between operations  13.5 us (10%)
  local copies, waits for them, and re-layouts  5.44 us (4%)
    psum x1, waiting for transfers between devices, shards(): full_sum, full_accum = lax.psum((prefix_sum, prefix_accum), 'ctx')  32 us
    dot_general x2, matrix products, block_terms(): jnp.einsum('rkgd,pkd->rkgp', row_block, prefix_keys, preferred_element_ty...  12.7 us
    reduce_sum x2, other arithmetic, block_terms(): sums_now = jnp.sum(weights, axis=-1, dtype=jnp.float32)  12.3 us
    dot_general x2, matrix products, block_terms(): jnp.einsum('rkgp,pkd->rkgd', weights, prefix_values, preferred_element_ty...  11.6 us
    pmax x1, blocking collectives, shards(): row_top = lax.pmax(merged_top, 'ctx')  11.2 us
    psum x1, blocking collectives, shards(): full_sum, full_accum = lax.psum((prefix_sum, prefix_accum), 'ctx')  10.9 us
    all_gather x1, blocking collectives, shards(): every_query = lax.all_gather(queries, 'ctx', axis=0, tiled=True)  10.4 us
    dot_general x1, matrix products, shards(): jnp.einsum('rkgs,rskd->rkgd', weights, suffix_values, preferred_element_t...  7.14 us
  transfers between devices with their start and end apart: 1, of which 1 were waited for; matrix products, arithmetic and copies ran while one was open for 1% of the time, Pallas kernels for 0%

commit v1 on v0

v1 whole, which is shorter than its diff:
```python
import functools
import math

import jax
import jax.numpy as jnp
from jax import lax
from jax.experimental import pallas as pl
from jax.experimental.pallas import tpu as pltpu
from jax.sharding import PartitionSpec as P

F32 = jnp.float32
BF16 = jnp.bfloat16
MASKED = -1e30
LANES = 128


def dot_t(a, b):
    return lax.dot_general(a, b, (((1,), (1,)), ((), ())), preferred_element_type=F32)


def kernel(
    n_ctx, tile_rows, first_tiles,
    len_ref, q_hbm, pk_hbm, pv_hbm, sk_hbm, sv_hbm, out_ref,
    q_raw, qk, k_raw, v_raw, k_cut, v_cut, wide, sk, sv,
    part_acc, part_stat, got_acc, got_stat,
    own_acc, own_top, own_sum, suf_acc, suf_top, suf_sum,
    q_sem, kv_sem, suf_sem, q_send, q_recv, kv_send, kv_recv, p_send, p_recv,
):
    rows, heads, width = q_hbm.shape
    kv = k_cut.shape[1]
    group = heads // kv
    flat = rows * group
    pair = 2 if n_ctx % 2 == 0 else 1
    chips = n_ctx // pair
    blocks = pair
    factor = width ** (-0.5) * math.log2(math.e)
    tiles = rows // tile_rows
    slots = sk.shape[1]
    me = lax.axis_index("ctx")
    chip, core = me // pair, me % pair

    def device(chip_at, core_at):
        return {"ctx": chip_at * pair + core_at}

    def remote(src, dst, send, recv, target):
        return pltpu.make_async_remote_copy(
            src_ref=src, dst_ref=dst, send_sem=send, recv_sem=recv,
            device_id=target, device_id_type=pl.DeviceIdType.MESH,
        )

    q_copy = pltpu.make_async_copy(q_hbm, q_raw.at[0], q_sem)
    q_copy.start()
    kv_copies = [
        pltpu.make_async_copy(pk_hbm, k_raw.at[0], kv_sem.at[0]),
        pltpu.make_async_copy(pv_hbm, v_raw.at[0], kv_sem.at[1]),
    ]
    for copy in kv_copies:
        copy.start()

    def suffix_copies(tile):
        span = pl.ds(tile * tile_rows, tile_rows)
        return (
            pltpu.make_async_copy(sk_hbm.at[span], sk.at[span], suf_sem.at[tile, 0]),
            pltpu.make_async_copy(sv_hbm.at[span], sv.at[span], suf_sem.at[tile, 1]),
        )

    partners = [device(lax.rem(chip + t, chips), core) for t in range(1, chips)]
    backs = [device(lax.rem(chip - t + chips, chips), core) for t in range(1, chips)]
    twin = device(chip, pair - 1 - core)
    greeted = partners + ([twin] if pair == 2 else [])
    if greeted:
        barrier = pltpu.get_barrier_semaphore()
        for target in greeted:
            pl.semaphore_signal(
                barrier, inc=1, device_id=target, device_id_type=pl.DeviceIdType.MESH
            )
        pl.semaphore_wait(barrier, len(greeted))

    q_sends = [
        remote(q_hbm, q_raw.at[t + 1], q_send.at[t], q_recv.at[t], partners[t])
        for t in range(chips - 1)
    ]
    for copy in q_sends:
        copy.start()
    kv_sends = []
    if pair == 2:
        kv_sends = [
            remote(pk_hbm, k_raw.at[1], kv_send.at[0], kv_recv.at[0], twin),
            remote(pv_hbm, v_raw.at[1], kv_send.at[1], kv_recv.at[1], twin),
        ]
        for copy in kv_sends:
            copy.start()

    def start_tile(tile, carry):
        for copy in suffix_copies(tile):
            copy.start()
        return carry

    lax.fori_loop(0, tiles, start_tile, 0)

    def split_queries(slot):
        wide_q = q_raw[slot].astype(F32).reshape(rows, kv, group, width)
        for k in range(kv):
            qk[slot, k] = wide_q[:, k].reshape(flat, width).astype(BF16)

    span = k_cut.shape[2]
    piece = wide.shape[1]
    pieces = span * kv // piece

    def split_block(block):
        def step(i, carry):
            at = pl.ds(pl.multiple_of(i * piece, piece), piece)
            to = pl.ds(pl.multiple_of(i * (piece // kv), piece // kv), piece // kv)
            wide[0] = k_raw[block, at, :].astype(F32)
            wide[1] = v_raw[block, at, :].astype(F32)
            for k in range(kv):
                rows_k = pl.ds(k, piece // kv, stride=kv) if kv > 1 else pl.ds(0, piece)
                k_cut[block, k, to, :] = wide[0, rows_k, :].astype(BF16)
                v_cut[block, k, to, 0:width] = wide[1, rows_k, :].astype(BF16)
                v_cut[block, k, to, width : 2 * width] = jnp.ones((piece // kv, width), BF16)
            return carry

        lax.fori_loop(0, pieces, step, 0)

    step_rows = LANES

    def block_terms(slot, k, block, at):
        scores = dot_t(qk[slot, k, at, :], k_cut[block, k]) * factor
        top = jnp.max(scores, axis=1, keepdims=True)
        weights = jnp.exp2(scores - top).astype(BF16)
        both = jnp.dot(weights, v_cut[block, k], preferred_element_type=F32)
        return top, both[:, :width], both[:, width:]

    def merge(one, two):
        top = jnp.maximum(one[0], two[0])
        a, b = jnp.exp2(one[0] - top), jnp.exp2(two[0] - top)
        return top, one[1] * a + two[1] * b, one[2] * a + two[2] * b

    chunks = flat // step_rows

    def own_block(block):
        def step(k, carry):
            for c in range(chunks):
                at = pl.ds(c * step_rows, step_rows)
                terms = block_terms(0, k, block, at)
                if block > 0:
                    terms = merge(terms, (own_top[k, at, :], own_acc[k, at, :], own_sum[k, at, :]))
                own_top[k, at, :] = jnp.broadcast_to(terms[0], (step_rows, width))
                own_acc[k, at, :] = terms[1]
                own_sum[k, at, :] = terms[2]
            return carry

        lax.fori_loop(0, kv, step, 0)

    diagonal = lax.broadcasted_iota(jnp.int32, (step_rows, LANES), 0) == lax.broadcasted_iota(
        jnp.int32, (step_rows, LANES), 1
    )

    def partial_copies(t, k):
        return (
            remote(part_acc.at[t, k], got_acc.at[t, k], p_send.at[t, k, 0], p_recv.at[t, k, 0], backs[t]),
            remote(part_stat.at[t, k], got_stat.at[t, k], p_send.at[t, k, 1], p_recv.at[t, k, 1], backs[t]),
        )

    def remote_rows(t):
        for k in range(kv):
            stat = []
            for c in range(chunks):
                at = pl.ds(c * step_rows, step_rows)
                terms = block_terms(t + 1, k, 0, at)
                for block in range(1, blocks):
                    terms = merge(terms, block_terms(t + 1, k, block, at))
                part_acc[t, k, at, :] = terms[1]
                top_wide = jnp.broadcast_to(terms[0], (step_rows, LANES))
                for i, x in enumerate((top_wide, terms[2])):
                    row = 2 * c + i
                    part_stat[t, k, row : row + 1, :] = jnp.sum(
                        jnp.where(diagonal, x, 0.0), axis=0, keepdims=True
                    )
            for copy in partial_copies(t, k):
                copy.start()

    column = lax.broadcasted_iota(jnp.int32, (heads, slots), 1)
    same_head = column % kv == lax.broadcasted_iota(jnp.int32, (heads, slots), 0) // group

    def suffix_tile(tile, carry):
        for copy in suffix_copies(tile):
            copy.wait()
        for i in range(tile_rows):
            r = tile * tile_rows + i
            live = same_head & (column < len_ref[r] * kv)
            scores = jnp.where(live, dot_t(q_raw[0, r], sk[r]) * factor, MASKED)
            top = jnp.max(scores, axis=1, keepdims=True)
            weights = jnp.exp2(scores - top).astype(BF16)
            total = jnp.sum(weights.astype(F32), axis=1, keepdims=True)
            acc = jnp.dot(weights, sv[r], preferred_element_type=F32)
            top = jnp.broadcast_to(top, (heads, width))
            total = jnp.broadcast_to(total, (heads, width))
            to = pl.ds(pl.multiple_of(r * group, group), group)
            for k in range(kv):
                part = slice(k * group, (k + 1) * group)
                suf_acc[k, to, :] = acc[part]
                suf_top[k, to, :] = top[part]
                suf_sum[k, to, :] = total[part]
        return carry

    q_copy.wait()
    split_queries(0)
    for copy in kv_copies:
        copy.wait()
    split_block(0)
    own_block(0)
    lax.fori_loop(0, first_tiles, suffix_tile, 0)
    for copy in kv_sends:
        copy.wait_recv()
    for block in range(1, blocks):
        split_block(block)
    for t in range(chips - 1):
        q_sends[t].wait_recv()
        split_queries(t + 1)
        remote_rows(t)
    for block in range(1, blocks):
        own_block(block)
    lax.fori_loop(first_tiles, tiles, suffix_tile, 0)

    for k in range(kv):
        for t in range(chips - 1):
            for copy in partial_copies(t, k):
                copy.wait_recv()
    per = step_rows // group
    for c in range(chunks):
        at = pl.ds(c * step_rows, step_rows)
        done = []
        for k in range(kv):
            terms = merge(
                (own_top[k, at, :], own_acc[k, at, :], own_sum[k, at, :]),
                (suf_top[k, at, :], suf_acc[k, at, :], suf_sum[k, at, :]),
            )
            for t in range(chips - 1):
                stats = []
                for i in range(2):
                    row = jnp.broadcast_to(
                        got_stat[t, k, 2 * c + i : 2 * c + i + 1, :], (step_rows, LANES)
                    )
                    stats.append(jnp.sum(jnp.where(diagonal, row, 0.0), axis=1, keepdims=True))
                terms = merge(terms, (stats[0], got_acc[t, k, at, :], stats[1]))
            done.append((terms[1] / terms[2]).reshape(per, 1, group, width))
        joined = jnp.concatenate(done, axis=1).reshape(per, heads, width)
        out_ref[c * per : (c + 1) * per] = joined.astype(BF16)
    for copy in q_sends + kv_sends:
        copy.wait_send()
    for t in range(chips - 1):
        for k in range(kv):
            for copy in partial_copies(t, k):
                copy.wait_send()


def shards(n_ctx, queries, prefix_keys, prefix_values, suffix_keys, suffix_values, lengths):
    rows, heads, width = queries.shape
    positions, kv, _ = prefix_keys.shape
    slots = suffix_keys.shape[1] * kv
    flat = rows * (heads // kv)
    pair = 2 if n_ctx % 2 == 0 else 1
    others = max(1, n_ctx // pair - 1)
    tile_rows = math.gcd(rows, 4)
    tiles = rows // tile_rows
    first_tiles = tiles // 3
    stat_rows = -(-2 * (flat // LANES) // 8) * 8
    piece = math.gcd(positions * kv, 1024)
    anywhere = pl.BlockSpec(memory_space=pl.ANY)
    vmem = pltpu.VMEM
    dma = pltpu.SemaphoreType.DMA
    call = pl.pallas_call(
        functools.partial(kernel, n_ctx, tile_rows, first_tiles),
        out_shape=jax.ShapeDtypeStruct((rows, heads, width), BF16),
        in_specs=[pl.BlockSpec(memory_space=pltpu.SMEM)] + [anywhere] * 5,
        out_specs=pl.BlockSpec(memory_space=vmem),
        scratch_shapes=[
            vmem((1 + others, rows, heads, width), BF16),
            vmem((1 + others, kv, flat, width), BF16),
            vmem((pair, positions * kv, width), BF16),
            vmem((pair, positions * kv, width), BF16),
            vmem((pair, kv, positions, width), BF16),
            vmem((pair, kv, positions, 2 * width), BF16),
            vmem((2, piece, width), F32),
            vmem((rows, slots, width), BF16),
            vmem((rows, slots, width), BF16),
            vmem((others, kv, flat, width), F32),
            vmem((others, kv, stat_rows, LANES), F32),
            vmem((others, kv, flat, width), F32),
            vmem((others, kv, stat_rows, LANES), F32),
        ]
        + [vmem((kv, flat, width), F32)] * 6
        + [
            dma,
            dma((2,)),
            dma((tiles, 2)),
            dma((others,)),
            dma((others,)),
            dma((2,)),
            dma((2,)),
            dma((others, kv, 2)),
            dma((others, kv, 2)),
        ],
        compiler_params=pltpu.CompilerParams(
            collective_id=0, has_side_effects=True, vmem_limit_bytes=62 * 1024 * 1024
        ),
    )
    return call(
        lengths,
        queries,
        prefix_keys.reshape(positions * kv, width),
        prefix_values.reshape(positions * kv, width),
        suffix_keys.reshape(rows, slots, width),
        suffix_values.reshape(rows, slots, width),
    )


def solution(mesh):
    placed = (
        P(("groups", "ctx"), "head", None),
        P(("groups", "ctx"), "head", None),
        P(("groups", "ctx"), "head", None),
        P(("groups", "ctx"), None, "head", None),
        P(("groups", "ctx"), None, "head", None),
        P(("groups", "ctx")),
    )
    return jax.shard_map(
        functools.partial(shards, mesh.shape["ctx"]),
        mesh=mesh,
        in_specs=placed,
        out_specs=P(("groups", "ctx"), "head", None),
        check_vma=False,
    )
```

time: 137 us -> 34.8 us (0.25)
  matrix products: 38.1 us -> 0 us
  Pallas kernels: 0 us -> 33 us
  blocking collectives: 32.5 us -> 0 us
  waiting for transfers between devices: 32 us -> 0 us
  other arithmetic: 14.7 us -> 0 us
  between operations: 13.5 us -> 0.01 us
  local copies, waits for them, and re-layouts: 5.44 us -> 1.62 us
    dot_general x6 -> x0, matrix products: 38.1 us -> none  [the longest x2 12.7 us: block_terms(): jnp.einsum('rkgd,pkd->rkgp', row_block, prefix_keys, preferred_element_ty...]
    pallas_call x0 -> x1, Pallas kernels: none -> 33 us  [shards(): call(lengths, queries, prefix_keys.reshape(positions * kv, width), prefix...]
    psum x1 -> x0, waiting for transfers between devices: 32 us -> none  [shards(): full_sum, full_accum = lax.psum((prefix_sum, prefix_accum), 'ctx')]
    reduce_sum x3 -> x0, other arithmetic: 12.9 us -> none  [the longest x2 12.3 us: block_terms(): sums_now = jnp.sum(weights, axis=-1, dtype=jnp.float32)]
    pmax x1 -> x0, blocking collectives: 11.2 us -> none  [shards(): row_top = lax.pmax(merged_top, 'ctx')]
    psum x1 -> x0, blocking collectives: 10.9 us -> none  [shards(): full_sum, full_accum = lax.psum((prefix_sum, prefix_accum), 'ctx')]
    all_gather x1 -> x0, blocking collectives: 10.4 us -> none  [shards(): every_query = lax.all_gather(queries, 'ctx', axis=0, tiled=True)]
    while x10 -> x0, local copies, waits for them, and re-layouts: 3.89 us -> none
  transfers between devices with their start and end apart: 1 -> 0, of which waited for: 1 -> 0; matrix products, arithmetic and copies ran while one was open for 1% -> 0% of each run, Pallas kernels for 0% -> 0%
where the time goes in v1:
time: 34.8 us; the launch traced here: 34.7 us
  Pallas kernels  33 us (95%)
  local copies, waits for them, and re-layouts  1.62 us (5%)
    pallas_call x1, Pallas kernels, shards(): call(lengths, queries, prefix_keys.reshape(positions * kv, width), prefix...  33 us
    unnamed x1, local copies, waits for them, and re-layouts  1.62 us

profile of v1, /device:TPU:0, one launch (start us, length us, event | category | flops | bytes accessed | tf_op | source)
XLA Modules:
  0.0 34.7 jit_solution(14721228325990595025)
XLA Ops:
  0.0 33.0 %shard_map.64 = bf16[48,16,128]{2,1,0:T(8,128)(2,1)} custom-call(s32[48]{0:T(128)} %len_ref.1, bf16[48,16,128]{2,1,0:T(8,128)(2,1)} %q_hbm.1, bf16[4096,128]{1,0:T(8,128)(2,1)} %bitcast.6, bf16[4096,128]{1,0:T(8,128)(2,1)} %bitcast.7, bf16[48,1024,128]{2,1,0:T(8,128)(2,1)} %bitcast.4, bf16[48,1024,128]{2,1,0:T(8,128)(2,1)} %bitcast.5), custom_call_target="tpu_custom_call" | custom-call | tf_op jit(solution)/shard_map/pallas_call | solution.py:309
  33.0 1.6 %copy.8 = bf16[48,16,128]{2,1,0:T(8,128)(2,1)} copy(bf16[48,16,128]{2,1,0:T(8,128)(2,1)} %shard_map.64) | data formatting | bytes 393216

commit v2 on v1

--- a/solution.py
+++ b/solution.py
@@ -21,7 +21,7 @@
 def kernel(
     n_ctx, tile_rows, first_tiles,
     len_ref, q_hbm, pk_hbm, pv_hbm, sk_hbm, sv_hbm, out_ref,
-    q_raw, qk, k_raw, v_raw, k_cut, v_cut, wide, sk, sv,
+    q_raw, q_far, qk, k_raw, v_raw, k_cut, v_cut, wide, sk, sv,
     part_acc, part_stat, got_acc, got_stat,
     own_acc, own_top, own_sum, suf_acc, suf_top, suf_sum,
     q_sem, kv_sem, suf_sem, q_send, q_recv, kv_send, kv_recv, p_send, p_recv,
@@ -77,11 +77,18 @@
         pl.semaphore_wait(barrier, len(greeted))
 
     q_sends = [
-        remote(q_hbm, q_raw.at[t + 1], q_send.at[t], q_recv.at[t], partners[t])
+        [
+            remote(
+                q_hbm.at[:, k * group : (k + 1) * group, :], q_far.at[t, k],
+                q_send.at[t, k], q_recv.at[t, k], partners[t],
+            )
+            for k in range(kv)
+        ]
         for t in range(chips - 1)
     ]
-    for copy in q_sends:
-        copy.start()
+    for k in range(kv):
+        for copies in q_sends:
+            copies[k].start()
     kv_sends = []
     if pair == 2:
         kv_sends = [
@@ -98,10 +105,10 @@
 
     lax.fori_loop(0, tiles, start_tile, 0)
 
-    def split_queries(slot):
-        wide_q = q_raw[slot].astype(F32).reshape(rows, kv, group, width)
+    def split_queries():
+        wide_q = q_raw[0].astype(F32).reshape(rows, kv, group, width)
         for k in range(kv):
-            qk[slot, k] = wide_q[:, k].reshape(flat, width).astype(BF16)
+            qk[0, k] = wide_q[:, k].reshape(flat, width).astype(BF16)
 
     span = k_cut.shape[2]
     piece = wide.shape[1]
@@ -156,15 +163,21 @@
         jnp.int32, (step_rows, LANES), 1
     )
 
+    def partial_copy(t, k, c):
+        if c == chunks:
+            src, dst = part_stat.at[t, k], got_stat.at[t, k]
+        else:
+            at = pl.ds(c * step_rows, step_rows)
+            src, dst = part_acc.at[t, k, at], got_acc.at[t, k, at]
+        return remote(src, dst, p_send.at[t, k, c], p_recv.at[t, k, c], backs[t])
+
     def partial_copies(t, k):
-        return (
-            remote(part_acc.at[t, k], got_acc.at[t, k], p_send.at[t, k, 0], p_recv.at[t, k, 0], backs[t]),
-            remote(part_stat.at[t, k], got_stat.at[t, k], p_send.at[t, k, 1], p_recv.at[t, k, 1], backs[t]),
-        )
+        return [partial_copy(t, k, c) for c in range(chunks + 1)]
 
     def remote_rows(t):
         for k in range(kv):
-            stat = []
+            q_sends[t][k].wait_recv()
+            qk[t + 1, k] = q_far[t, k].astype(F32).reshape(flat, width).astype(BF16)
             for c in range(chunks):
                 at = pl.ds(c * step_rows, step_rows)
                 terms = block_terms(t + 1, k, 0, at)
@@ -177,8 +190,8 @@
                     part_stat[t, k, row : row + 1, :] = jnp.sum(
                         jnp.where(diagonal, x, 0.0), axis=0, keepdims=True
                     )
-            for copy in partial_copies(t, k):
-                copy.start()
+                partial_copy(t, k, c).start()
+            partial_copy(t, k, chunks).start()
 
     column = lax.broadcasted_iota(jnp.int32, (heads, slots), 1)
     same_head = column % kv == lax.broadcasted_iota(jnp.int32, (heads, slots), 0) // group
@@ -205,7 +218,7 @@
         return carry
 
     q_copy.wait()
-    split_queries(0)
+    split_queries()
     for copy in kv_copies:
         copy.wait()
     split_block(0)
@@ -216,8 +229,6 @@
     for block in range(1, blocks):
         split_block(block)
     for t in range(chips - 1):
-        q_sends[t].wait_recv()
-        split_queries(t + 1)
         remote_rows(t)
     for block in range(1, blocks):
         own_block(block)
@@ -247,7 +258,7 @@
             done.append((terms[1] / terms[2]).reshape(per, 1, group, width))
         joined = jnp.concatenate(done, axis=1).reshape(per, heads, width)
         out_ref[c * per : (c + 1) * per] = joined.astype(BF16)
-    for copy in q_sends + kv_sends:
+    for copy in sum(q_sends, []) + kv_sends:
         copy.wait_send()
     for t in range(chips - 1):
         for k in range(kv):
@@ -264,7 +275,7 @@
     others = max(1, n_ctx // pair - 1)
     tile_rows = math.gcd(rows, 4)
     tiles = rows // tile_rows
-    first_tiles = tiles // 3
+    first_tiles = tiles // 6
     stat_rows = -(-2 * (flat // LANES) // 8) * 8
     piece = math.gcd(positions * kv, 1024)
     anywhere = pl.BlockSpec(memory_space=pl.ANY)
@@ -276,7 +287,8 @@
         in_specs=[pl.BlockSpec(memory_space=pltpu.SMEM)] + [anywhere] * 5,
         out_specs=pl.BlockSpec(memory_space=vmem),
         scratch_shapes=[
-            vmem((1 + others, rows, heads, width), BF16),
+            vmem((1, rows, heads, width), BF16),
+            vmem((others, kv, rows, heads // kv, width), BF16),
             vmem((1 + others, kv, flat, width), BF16),
             vmem((pair, positions * kv, width), BF16),
             vmem((pair, positions * kv, width), BF16),
@@ -295,12 +307,12 @@
             dma,
             dma((2,)),
             dma((tiles, 2)),
-            dma((others,)),
-            dma((others,)),
+            dma((others, kv)),
+            dma((others, kv)),
             dma((2,)),
             dma((2,)),
-            dma((others, kv, 2)),
-            dma((others, kv, 2)),
+            dma((others, kv, flat // LANES + 1)),
+            dma((others, kv, flat // LANES + 1)),
         ],
         compiler_params=pltpu.CompilerParams(
             collective_id=0, has_side_effects=True, vmem_limit_bytes=62 * 1024 * 1024

time: 34.8 us -> 37.2 us (1.069)
  Pallas kernels: 33 us -> 35.4 us
    pallas_call x1, Pallas kernels: 33 us -> 35.4 us  [shards(): call(lengths, queries, prefix_keys.reshape(positions * kv, width), prefix...]
where the time goes in v2:
time: 37.2 us; the launch traced here: 37 us
  Pallas kernels  35.4 us (95%)
  local copies, waits for them, and re-layouts  1.62 us (4%)
    pallas_call x1, Pallas kernels, shards(): call(lengths, queries, prefix_keys.reshape(positions * kv, width), prefix...  35.4 us
    unnamed x1, local copies, waits for them, and re-layouts  1.62 us

profile of v2, /device:TPU:0, one launch (start us, length us, event | category | flops | bytes accessed | tf_op | source)
XLA Modules:
  0.0 37.0 jit_solution(3194467008954667962)
XLA Ops:
  0.0 35.4 %shard_map.64 = bf16[48,16,128]{2,1,0:T(8,128)(2,1)} custom-call(s32[48]{0:T(128)} %len_ref.1, bf16[48,16,128]{2,1,0:T(8,128)(2,1)} %q_hbm.1, bf16[4096,128]{1,0:T(8,128)(2,1)} %bitcast.6, bf16[4096,128]{1,0:T(8,128)(2,1)} %bitcast.7, bf16[48,1024,128]{2,1,0:T(8,128)(2,1)} %bitcast.4, bf16[48,1024,128]{2,1,0:T(8,128)(2,1)} %bitcast.5), custom_call_target="tpu_custom_call" | custom-call | tf_op jit(solution)/shard_map/pallas_call | solution.py:321
  35.4 1.6 %copy.8 = bf16[48,16,128]{2,1,0:T(8,128)(2,1)} copy(bf16[48,16,128]{2,1,0:T(8,128)(2,1)} %shard_map.64) | data formatting | bytes 393216
